TPU v7x, 32 devices: a whole 2x2x4 slice. The times are simulated.
32 devices in a mesh: pair: 8 (over z, x), sector: 4 (over y, core).
Axes of the slice: x: 2, y: 2, z: 4, core: 2. Of those that a mesh axis runs over, the one named last changes fastest.
Arguments:
- wave: bfloat16 [4, 1024, 1024], P('sector', 'pair'), may hold values from -6 to 6
- left_ops: bfloat16 [16, 4, 1024, 1024], P('pair', 'sector'), may hold values from -0.1875 to 0.1875
- right_ops: bfloat16 [16, 4, 1024, 1024], P('pair', 'sector'), may hold values from -0.046875 to 0.046875
- targets: int32 [16, 4], P('pair', 'sector'), may hold values from -1 to 3
- sector_sizes: int32 [4], replicated, may hold values from 256 to 1024
- pair_ids: int32 [16], P('pair'), may hold values from 0 to 15, each once
- pair_coefficients: float32 [16], replicated, may hold values from 0.25 to 2
Outputs:
- sigma_blocks: float32 [4, 1024, 1024], P('sector', 'pair')
Inputs may be any that keep to these rules, and one draw needn't show every extreme that they name: `pair_ids`: each orbital pair once.
All inputs are finite; a program needn't handle non-finite values.
Results may differ from a plain program's by a relative error of at most 0.0029.
Values may be sent and summed in bfloat16 or wider, within the bound.
A program may use at most 128 MiB of HBM per device.

v0:
```python
import jax
import jax.numpy as jnp
from jax import lax
from jax.sharding import PartitionSpec as P


def body(wave, left_ops, right_ops, targets, sector_sizes, pair_ids, pair_coefficients):
    block = wave.shape[2]
    local_rows = wave.shape[1]
    pair_slots = left_ops.shape[0]
    sectors = sector_sizes.shape[0]
    pair_count = lax.axis_size("pair")
    own_sector = lax.axis_index("sector")
    sector_ids = jnp.arange(sectors, dtype=jnp.int32)
    own_size = jnp.sum(jnp.where(sector_ids == own_sector, sector_sizes, 0))
    col_ids = jnp.arange(block, dtype=jnp.int32)
    row_ids = lax.axis_index("pair") * local_rows + jnp.arange(local_rows, dtype=jnp.int32)
    col_used = col_ids < own_size
    row_used = row_ids < own_size
    masked = wave[0] * (row_used[:, None] & col_used[None, :]).astype(wave.dtype)
    table_ids = jnp.arange(pair_coefficients.shape[0], dtype=jnp.int32)
    factor = jnp.sum(
        jnp.where(pair_ids[:, None] == table_ids[None, :], pair_coefficients[None, :], 0.0), axis=1
    )
    left_mats = left_ops[:, 0]
    right_mats = right_ops[:, 0]
    chosen_targets = targets[:, 0]
    totals = jnp.zeros((sectors, block, block), jnp.float32)
    gathered = lax.all_gather(masked, "pair", axis=0, tiled=True)
    for member in range(pair_slots):
        target = chosen_targets[member]
        left_mat = left_mats[member]
        right_mat = right_mats[member]
        weight = factor[member]

        def present_term(left_mat=left_mat, right_mat=right_mat, weight=weight):
            left = jnp.dot(left_mat, gathered, preferred_element_type=jnp.float32).astype(
                jnp.bfloat16
            )
            term = lax.dot_general(
                left, right_mat, (((1,), (1,)), ((), ())), preferred_element_type=jnp.float32
            )
            return weight * term

        def absent_term():
            return jnp.zeros((block, block), jnp.float32)

        addition = lax.cond(target >= 0, present_term, absent_term)
        place = jnp.maximum(target, 0)
        current = lax.dynamic_index_in_dim(totals, place, 0, keepdims=False)
        totals = lax.dynamic_update_index_in_dim(totals, current + addition, place, 0)
    arranged = totals.reshape(sectors, pair_count, local_rows, block).transpose(1, 0, 2, 3)
    arranged = arranged.reshape(pair_count * sectors * local_rows, block)
    summed = lax.psum_scatter(arranged, ("pair", "sector"), scatter_dimension=0, tiled=True)[None]
    out_mask = (row_used[:, None] & col_used[None, :]).astype(jnp.float32)
    return summed * out_mask[None]


def solution(mesh):
    placed = (
        P("sector", "pair", None),
        P("pair", "sector", None, None),
        P("pair", "sector", None, None),
        P("pair", "sector"),
        P(),
        P("pair"),
        P(),
    )
    return jax.shard_map(
        body, mesh=mesh, in_specs=placed, out_specs=P("sector", "pair", None), check_vma=False
    )
```

profile of v0, /device:TPU:1, one launch (start us, length us, event | category | flops | bytes accessed | tf_op | source)
XLA Modules:
  0.0 303.4 jit_solution(10852317030803112737)
XLA Ops:
  6.5 0.0 all-gather.2.cloned.1.call-start
  6.5 1.3 fusion.22
  7.8 0.6 iota_compare_fusion
  8.5 0.7 add_compare_fusion
  9.1 1.8 and_select_fusion.1
  11.0 0.0 all-gather.2.cloned.1.call-update
  11.0 0.0 reduce-scatter.2.cloned.1.call-start
  11.0 1.3 fusion.23
  14.8 0.9 fusion.21
  15.7 44.7 %all-gather.2.cloned.1.call-done = bf16[1024,1024]{1,0:T(8,128)(2,1)} async-done(((bf16[128,1024]{1,0:T(8,128)(2,1)}), bf16[1024,1024]{1,0:T(8,128)(2,1)}) %all-gather.2.cloned.1.call-update) | async-done | bytes 2097168 | tf_op jit(solution)/shard_map/all_gather | solution.py:29
  60.4 9.3 %conditional.2 = (f32[1,1024,1024]{2,1,0:T(8,128)}) conditional(s32[]{:T(128)} %bitcast.7, () %tuple.19, (f32[2]{0:T(128)S(1)}, bf16[2,1,1024,1024]{3,2,1,0:T(8,128)(2,1)}, bf16[1024,1024]{1,0:T(8,128)(2,1)}, bf16[2,1,1024,1024]{3,2,1,0:T(8,128)(2,1)}) %tuple.20), branch_computations={%region_2.3_spmd, %region_3.4_spmd} | conditional | flops 4297064448 | bytes 10485772 | solution.py:48
  60.4 9.3 %multiply_bitcast_fusion = f32[1,1024,1024]{2,1,0:T(8,128)} fusion(bf16[2,1,1024,1024]{3,2,1,0:T(8,128)(2,1)} %get-tuple-element.43, f32[]{:T(128)S(1)} %bitcast.48, bf16[1024,1024]{1,0:T(8,128)(2,1)} %get-tuple-element.42, bf16[2,1,1024,1024]{3,2,1,0:T(8,128)(2,1)} %get-tuple-element.41), kind=kOutput, calls=%fused_computation | convolution fusion | flops 4297064448 | bytes 10485764 | tf_op jit(solution)/shard_map/cond/branch_1_fun/dot_general | solution.py:40
  69.7 0.0 copy-start.1
  69.7 2.1 broadcast_in_dim.40
  71.9 0.0 copy-done.1
  71.9 0.6 constant_dynamic-update-slice_fusion
  72.6 0.0 copy-start
  72.6 5.7 %copy-done = f32[4,1024,1024]{2,1,0:T(8,128)} copy-done((f32[4,1024,1024]{2,1,0:T(8,128)}, f32[4,1024,1024]{2,1,0:T(8,128)S(1)}, u32[]{:S(2)}) %copy-start) | copy-done | bytes 16777240
  78.3 2.2 constant_dynamic-slice_fusion
  80.5 2.5 conditional.3
  80.5 2.5 broadcast.26
  83.0 6.8 %bitcast_dynamic-update-slice_fusion = f32[4,1024,1024]{2,1,0:T(8,128)} fusion(f32[4,1024,1024]{2,1,0:T(8,128)} %copy-done, s32[]{:T(128)} %bitcast.10, f32[1024,1024]{1,0:T(8,128)} %get-tuple-element.51, f32[1,1024,1024]{2,1,0:T(8,128)} %constant_dynamic-slice_fusion), kind=kLoop, calls=%fused_computation.14 | loop fusion | flops 1048576 | bytes 12583424 | tf_op jit(solution)/shard_map/jit(dynamic_update_index_in_dim)/dynamic_update_slice | solution.py:51
  89.8 11.8 %copy.9 = f32[8,4,128,1024]{3,2,1,0:T(8,128)} copy(f32[8,4,128,1024]{3,2,0,1:T(8,128)} %bitcast.45) | data formatting | bytes 33554432 | tf_op jit(solution)/shard_map/transpose | solution.py:52
  101.6 0.0 reduce-scatter.2.cloned.1.call-update
  101.6 193.0 %reduce-scatter.2.cloned.1.call-done = f32[128,1024]{1,0:T(8,128)} async-done(((f32[4096,1024]{1,0:T(8,128)}), f32[128,1024]{1,0:T(8,128)}) %reduce-scatter.2.cloned.1.call-update) | async-done | bytes 524304 | tf_op jit(solution)/shard_map/reduce_scatter | solution.py:54
  294.6 2.0 fusion.20
Async XLA Ops:
  6.5 53.9 %all-gather.2.cloned.1.call-start = ((), (), s32[]{:S(2)}) async-start(), calls=%async_computation.1 | async-start | bytes 2359296 | tf_op jit(solution)/shard_map/all_gather | solution.py:29
  11.0 283.6 %reduce-scatter.2.cloned.1.call-start = ((), (), s32[]{:S(2)}) async-start(), calls=%async_computation.2 | async-start | bytes 17301504 | tf_op jit(solution)/shard_map/reduce_scatter | solution.py:54
  69.7 2.2 copy-start.1
  72.6 5.7 %copy-start = (f32[4,1024,1024]{2,1,0:T(8,128)}, f32[4,1024,1024]{2,1,0:T(8,128)S(1)}, u32[]{:S(2)}) copy-start(f32[4,1024,1024]{2,1,0:T(8,128)S(1)} %constant_dynamic-update-slice_fusion) | copy-start | bytes 50331652
Sparse Core Ops, SparseCore 0:
  11.1 49.2 all-gather.1
  101.7 192.7 reduce-scatter.1
where the time goes:
time: 304 us; the launch traced here: 303 us
  waiting for transfers between devices  238 us (78%)
  local copies, waits for them, and re-layouts  26.4 us (9%)
  between operations  15.9 us (5%)
  other arithmetic  14 us (5%)
  matrix products  9.33 us (3%)
    reduce_scatter x1, waiting for transfers between devices, body(): lax.psum_scatter(arranged, ('pair', 'sector'), scatter_dimension=0, tiled...  193 us
    all_gather x1, waiting for transfers between devices, body(): gathered = lax.all_gather(masked, 'pair', axis=0, tiled=True)  44.7 us
    transpose x1, local copies, waits for them, and re-layouts, body(): totals.reshape(sectors, pair_count, local_rows, block).transpose(1, 0, 2, 3)  11.8 us
    dot_general x1, matrix products, present_term(): lax.dot_general(left, right_mat, (((1,), (1,)), ((), ())), preferred_elem...  9.33 us
    dynamic_update_slice x1, other arithmetic, body(): lax.dynamic_update_index_in_dim(totals, current + addition, place, 0)  6.77 us
  transfers between devices with their start and end apart: 2, of which 2 were waited for; matrix products, arithmetic and copies ran while one was open for 1% of the time, Pallas kernels for 0%

commit v1 on v0

v1 whole, which is shorter than its diff:
```python
import functools

import jax
import jax.numpy as jnp
from jax import lax
from jax.experimental import pallas as pl
from jax.experimental.pallas import tpu as pltpu
from jax.sharding import PartitionSpec as P

MESH = pl.DeviceIdType.MESH
F32 = jnp.float32
LANES = 128
PLANE_DEPTH = 128
ROW_TILE = 256


def step_kernel(
    cfg, wave_ref, weight_ref, left_hbm, right_hbm, out_ref,
    wbuf, lbuf, rbuf, acc, left, own, psend, precv, wother,
    xs, xr, ys, yr, zs, zup, zdn, fsend, frecv, load_sem, sems_s, sems_r, line_s, line_r, gat_s, gat_r,
):
    Z, X, T, K, rows, block, groups, orders = cfg
    half = block // 2
    pair, sector = lax.axis_index("pair"), lax.axis_index("sector")
    z, x = pair // X, lax.rem(pair, X)
    y, c = sector // 2, lax.rem(sector, 2)

    def dev(zz=None, xx=None, yy=None, cc=None):
        zz, xx = z if zz is None else zz, x if xx is None else xx
        yy, cc = y if yy is None else yy, c if cc is None else cc
        return (zz * X + xx, yy * 2 + cc)

    x_dev, y_dev, c_dev = dev(xx=1 - x), dev(yy=1 - y), dev(cc=1 - c)
    up_dev, dn_dev = dev(zz=z + 1), dev(zz=z - 1)
    has_up, has_dn = z + 1 < Z, z >= 1

    loads = []
    for k in range(K):
        loads.append(pltpu.make_async_copy(left_hbm.at[k], lbuf.at[k], load_sem.at[k]))
        loads.append(pltpu.make_async_copy(right_hbm.at[k], rbuf.at[k], load_sem.at[K + k]))
    for k in range(K):
        loads[2 * k].start()

    barrier = pltpu.get_barrier_semaphore()
    for other in (x_dev, y_dev, c_dev):
        pl.semaphore_signal(barrier, inc=1, device_id=other, device_id_type=MESH)

    @pl.when(has_up)
    def _():
        pl.semaphore_signal(barrier, inc=1, device_id=up_dev, device_id_type=MESH)

    @pl.when(has_dn)
    def _():
        pl.semaphore_signal(barrier, inc=1, device_id=dn_dev, device_id_type=MESH)

    pl.semaphore_wait(barrier, 3 + has_up.astype(jnp.int32) + has_dn.astype(jnp.int32))

    def remote(src, dst, ss, rs, device):
        return pltpu.make_async_remote_copy(
            src_ref=src, dst_ref=dst, send_sem=ss, recv_sem=rs, device_id=device, device_id_type=MESH
        )

    def hop(q, way, src=None):
        device = (up_dev, dn_dev, x_dev)[way]
        src = wbuf.at[q, x] if src is None else src
        return remote(src, wbuf.at[q, x], gat_s.at[way, q], gat_r.at[q, x], device)

    def arrival(q, xx):
        return remote(wbuf.at[q, xx], wbuf.at[q, xx], gat_s.at[2, q], gat_r.at[q, xx], x_dev)

    @pl.when(has_up)
    def _():
        hop(z, 0, wave_ref).start()

    @pl.when(has_dn)
    def _():
        hop(z, 1, wave_ref).start()

    hop(z, 2, wave_ref).start()
    weights_copy = remote(weight_ref, wother, sems_s.at[0], sems_r.at[0], c_dev)
    weights_copy.start()
    for k in range(K):
        loads[2 * k + 1].start()

    for g in range(groups):
        @pl.when(jnp.logical_not(has_dn))
        def _(g=g):
            zup[g][z] = jnp.zeros(zup[g].shape[1:], zup[g].dtype)

        @pl.when(jnp.logical_not(has_up))
        def _(g=g):
            zdn[g][z] = jnp.zeros(zdn[g].shape[1:], zdn[g].dtype)

    depth = X * rows
    planewise = depth % PLANE_DEPTH == 0
    tile = min(ROW_TILE, block)
    tiles = block // tile

    def multiply(q, first):
        plane = wbuf.at[q]

        def one(i, carry):
            k, at = i // tiles, pl.multiple_of(lax.rem(i, tiles) * tile, tile)
            cols = pl.ds(pl.multiple_of(q * depth, depth), depth)
            product = jnp.dot(
                lbuf[k, pl.ds(at, tile), cols], plane[...].reshape(depth, block), preferred_element_type=F32
            )
            if first:
                acc[k, pl.ds(at, tile), :] = product
            else:
                acc[k, pl.ds(at, tile), :] += product
            return carry

        lax.fori_loop(0, K * tiles, one, 0)

    def take_plane(q):
        arrival(q, 1 - x).wait_recv()
        if planewise:
            multiply(q, False)

    wbuf[z, x] = wave_ref[...]
    for k in range(K):
        loads[2 * k].wait()

    def forward(d, carry):
        lo, hi = z - d, z + d

        @pl.when(lo >= 0)
        def _():
            arrival(lo, x).wait_recv()

            @pl.when(has_up)
            def _():
                hop(lo, 0).start()

            hop(lo, 2).start()

        @pl.when(hi < Z)
        def _():
            arrival(hi, x).wait_recv()

            @pl.when(has_dn)
            def _():
                hop(hi, 1).start()

            hop(hi, 2).start()

        @pl.when(d == 1)
        def _():
            arrival(z, 1 - x).wait_recv()
            if planewise:
                multiply(z, True)

        @pl.when(jnp.logical_and(d > 1, lo + 1 >= 0))
        def _():
            take_plane(lo + 1)

        @pl.when(jnp.logical_and(d > 1, hi - 1 < Z))
        def _():
            take_plane(hi - 1)

        return carry

    lax.fori_loop(1, Z, forward, 0)

    @pl.when(z == Z - 1)
    def _():
        take_plane(0)

    @pl.when(z == 0)
    def _():
        take_plane(Z - 1)

    def finish_left(i, carry):
        k, at = i // tiles, pl.multiple_of(lax.rem(i, tiles) * tile, tile)
        if planewise:
            value = acc[k, pl.ds(at, tile), :]
        else:
            value = jnp.dot(
                lbuf[k, pl.ds(at, tile), :], wbuf[...].reshape(block, block), preferred_element_type=F32
            )
        left[k, pl.ds(at, tile), :] = value.astype(jnp.bfloat16)
        return carry

    lax.fori_loop(0, K * tiles, finish_left, 0)
    for k in range(K):
        loads[2 * k + 1].wait()

    width = 2 * LANES

    def second(part, side, dest):
        def one(i, carry):
            k, at = i // tiles, pl.multiple_of(lax.rem(i, tiles) * tile, tile)
            right_at = pl.multiple_of(side * half + part * width, width)
            term = lax.dot_general(
                left[k, pl.ds(at, tile), :], rbuf[k, pl.ds(right_at, width), :],
                (((1,), (1,)), ((), ())), preferred_element_type=F32,
            )
            for j in range(2):
                dest[2 * part + j, k, pl.ds(at, tile), :] = term[:, j * LANES : (j + 1) * LANES].astype(dest.dtype)
            return carry

        lax.fori_loop(0, K * tiles, one, 0)

    def part_copy(part):
        span = pl.ds(2 * part, 2)
        return remote(psend.at[span], precv.at[span], sems_s.at[1 + part], sems_r.at[1 + part], c_dev)

    base = 1 + groups // 2

    def step_copy(g, number):
        letter = orders[g].replace("z", "")[number]
        s, r = ((xs, xr), (ys, yr))["xy".index(letter)]
        at = base + 2 * g + number
        return remote(s[g], r[g], sems_s.at[at], sems_r.at[at], x_dev if letter == "x" else y_dev)

    def chip_sum(g, ty, tc, zz, xx):
        at = pl.ds(pl.multiple_of((zz * X + xx) * rows, rows), rows)
        t = ty * 2 + tc
        total = None
        for k in range(K):
            mine = own[g, k, at, :] * weight_ref[k * T + t, 0:1, :]
            theirs = precv[g, k, at, :].astype(F32) * wother[k * T + t, 0:1, :]
            total = mine + theirs if total is None else total + mine + theirs
        return total

    def loop(count, f):
        def one(i, carry):
            f(i)
            return carry

        lax.fori_loop(0, count, one, 0)

    def x_first(g):
        def one(zz):
            for ty in range(2):
                for tc in range(2):
                    xs[g][ty, tc, zz] = chip_sum(g, ty, tc, zz, 1 - x).astype(jnp.bfloat16)
        loop(Z, one)
        step_copy(g, 0).start()

    def y_first(g):
        def one(zz):
            for tc in range(2):
                for xx in range(2):
                    ys[g][tc, zz, xx] = chip_sum(g, 1 - y, tc, zz, xx).astype(jnp.bfloat16)
        loop(Z, one)
        step_copy(g, 0).start()

    def y_second(g):
        step_copy(g, 0).wait_recv()

        def one(zz):
            for tc in range(2):
                value = chip_sum(g, 1 - y, tc, zz, x) + xr[g][1 - y, tc, zz].astype(F32)
                ys[g][tc, zz] = value.astype(jnp.bfloat16)
        loop(Z, one)
        step_copy(g, 1).start()

    def x_second(g):
        step_copy(g, 0).wait_recv()

        def one(zz):
            for tc in range(2):
                value = chip_sum(g, y, tc, zz, 1 - x) + yr[g][tc, zz, 1 - x].astype(F32)
                xs[g][tc, zz] = value.astype(jnp.bfloat16)
        loop(Z, one)
        step_copy(g, 1).start()

    def line_item(g, tc, zz):
        value = chip_sum(g, y, tc, zz, x)
        if orders[g][0] == "x":
            return value + xr[g][y, tc, zz].astype(F32) + yr[g][tc, zz].astype(F32)
        return value + yr[g][tc, zz, x].astype(F32) + xr[g][tc, zz].astype(F32)

    def line_values(g, zz):
        return {(tc,): line_item(g, tc, zz) for tc in range(2)}

    def line_copy(g, zz, way):
        dst = (zup, zdn)[way][g].at[zz]
        return remote(zs[g].at[zz], dst, line_s.at[g, zz], line_r.at[g, way, zz], (up_dev, dn_dev)[way])

    def line_step(g, j):
        for way, zz, active, middle in ((0, Z - 1 - j, Z - 1 - j > z, has_dn), (1, j, j < z, has_up)):
            @pl.when(active)
            def _(way=way, zz=zz, middle=middle):
                @pl.when(middle)
                def _():
                    line_copy(g, zz, way).wait_recv()
                    for at, value in line_values(g, zz).items():
                        arrived = (zup, zdn)[way][g][(zz,) + at]
                        zs[g][(zz,) + at] = (value + arrived.astype(F32)).astype(zs[g].dtype)

                @pl.when(jnp.logical_not(middle))
                def _():
                    for at, value in line_values(g, zz).items():
                        zs[g][(zz,) + at] = value.astype(zs[g].dtype)

                line_copy(g, zz, way).start()

    def line_all(chosen):
        loop(Z - 1, lambda j: [line_step(g, j) for g in chosen])

    def line_end(g):
        @pl.when(has_dn)
        def _():
            line_copy(g, z, 0).wait_recv()

        @pl.when(has_up)
        def _():
            line_copy(g, z, 1).wait_recv()

    def ended(g, at, value):
        return value + zup[g][(z,) + at].astype(F32) + zdn[g][(z,) + at].astype(F32)

    def final_copy(g):
        at = base + 2 * groups + g
        return remote(fsend.at[g], frecv.at[g], sems_s.at[at], sems_r.at[at], c_dev)

    def finish(g):
        def value(tc):
            return ended(g, (tc,), line_item(g, tc, z))

        line_end(g)
        fsend[g] = value(1 - c)
        final_copy(g).start()
        out_ref[c, g] = value(c)

    for part in range(groups // 2):
        second(part, 1 - c, psend)
        part_copy(part).start()
        second(part, c, own)
        if part == 0:
            weights_copy.wait_recv()
        part_copy(part).wait_recv()
        x_first(2 * part)
        y_first(2 * part + 1)
    def lines(part):
        for g in (2 * part, 2 * part + 1):
            step_copy(g, 1).wait_recv()
        line_all((2 * part, 2 * part + 1))

    for part in range(groups // 2):
        y_second(2 * part)
        x_second(2 * part + 1)
        if part:
            lines(part - 1)
    lines(groups // 2 - 1)
    for g in range(groups):
        finish(g)
    for g in range(groups):
        final_copy(g).wait_recv()
    out_ref[1 - c] = frecv[...]

    for q_way in range(3):
        def drain(q, q_way=q_way):
            sent = (
                jnp.logical_and(has_up, q <= z),
                jnp.logical_and(has_dn, q >= z),
                None,
            )[q_way]
            if sent is None:
                hop(q, q_way).wait_send()
            else:
                @pl.when(sent)
                def _():
                    hop(q, q_way).wait_send()
        loop(Z, drain)
    weights_copy.wait_send()
    for part in range(groups // 2):
        part_copy(part).wait_send()
    for g in range(groups):
        step_copy(g, 0).wait_send()
        step_copy(g, 1).wait_send()
        final_copy(g).wait_send()

        def drain_line(zz, g=g):
            @pl.when(zz > z)
            def _():
                line_copy(g, zz, 0).wait_send()

            @pl.when(zz < z)
            def _():
                line_copy(g, zz, 1).wait_send()
        loop(Z, drain_line)


def kernel_entry(cfg, *refs):
    groups = cfg[6]
    ins, scratch = refs[:5], list(refs[5:])
    plain = scratch[:9]
    per_group = [scratch[9 + n * groups : 9 + (n + 1) * groups] for n in range(7)]
    step_kernel(cfg, *ins, *plain, *per_group, *scratch[9 + 7 * groups :])


def body(wave, left_ops, right_ops, targets, sector_sizes, pair_ids, pair_coefficients):
    block = wave.shape[2]
    rows = wave.shape[1]
    K = left_ops.shape[0]
    T = sector_sizes.shape[0]
    pairs = lax.axis_size("pair")
    X = 2
    Z = pairs // X
    half = block // 2
    groups = half // LANES
    orders = tuple(("xyz", "yxz")[g % 2] for g in range(groups))
    own_sector = lax.axis_index("sector")
    sector_ids = jnp.arange(T, dtype=jnp.int32)
    own_size = jnp.sum(jnp.where(sector_ids == own_sector, sector_sizes, 0))
    col_ids = jnp.arange(block, dtype=jnp.int32)
    row_ids = lax.axis_index("pair") * rows + jnp.arange(rows, dtype=jnp.int32)
    used = (row_ids < own_size)[:, None] & (col_ids < own_size)[None, :]
    masked = wave[0] * used.astype(wave.dtype)
    table_ids = jnp.arange(pair_coefficients.shape[0], dtype=jnp.int32)
    factor = jnp.sum(
        jnp.where(pair_ids[:, None] == table_ids[None, :], pair_coefficients[None, :], 0.0), axis=1
    )
    weights = jnp.where(targets == sector_ids[None, :], factor[:, None], 0.0).reshape(K * T, 1, 1)
    weights = jnp.broadcast_to(weights, (K * T, 8, LANES)).astype(F32)

    bf = jnp.bfloat16
    line_type = bf if Z <= 4 else F32
    xs, xr, ys, yr, zs, zup, zdn = [], [], [], [], [], [], []
    for order in orders:
        tail = (rows, LANES)
        x_shape, y_shape, z_shape = {
            "x": ((2, 2, Z), (2, Z), (Z, 2)),
            "y": ((2, Z), (2, Z, X), (Z, 2)),
        }[order[0]]
        for where, shape, kind in (
            (xs, x_shape, bf), (xr, x_shape, bf), (ys, y_shape, bf), (yr, y_shape, bf),
            (zs, z_shape, line_type), (zup, z_shape, line_type), (zdn, z_shape, line_type),
        ):
            where.append(pltpu.VMEM(shape + tail, kind))
    count = 1 + groups // 2 + 3 * groups
    dma = pltpu.SemaphoreType.DMA
    cfg = (Z, X, T, K, rows, block, groups, orders)
    planewise = (X * rows) % PLANE_DEPTH == 0
    vmem, anywhere = pl.BlockSpec(memory_space=pltpu.VMEM), pl.BlockSpec(memory_space=pl.ANY)
    parts = pl.pallas_call(
        functools.partial(kernel_entry, cfg),
        out_shape=jax.ShapeDtypeStruct((2, groups, rows, LANES), F32),
        in_specs=[vmem, vmem, anywhere, anywhere],
        out_specs=vmem,
        scratch_shapes=[
            pltpu.VMEM((Z, X, rows, block), bf),
            pltpu.VMEM((K, block, block), bf),
            pltpu.VMEM((K, block, block), bf),
            pltpu.VMEM((K, block, block) if planewise else (8, LANES), F32),
            pltpu.VMEM((K, block, block), bf),
            pltpu.VMEM((groups, K, block, LANES), F32),
            pltpu.VMEM((groups, K, block, LANES), F32),
            pltpu.VMEM((groups, K, block, LANES), F32),
            pltpu.VMEM((K * T, 8, LANES), F32),
            *xs, *xr, *ys, *yr, *zs, *zup, *zdn,
            pltpu.VMEM((groups, rows, LANES), F32),
            pltpu.VMEM((groups, rows, LANES), F32),
            dma((2 * K,)), dma((count,)), dma((count,)),
            dma((groups, Z)), dma((groups, 2, Z)), dma((3, Z)), dma((Z, X)),
        ],
        compiler_params=pltpu.CompilerParams(
            collective_id=0, has_side_effects=True, vmem_limit_bytes=60 * 1024 * 1024
        ),
        name="sigma_step",
    )(masked, weights, left_ops[:, 0], right_ops[:, 0])
    summed = parts.transpose(2, 0, 1, 3).reshape(rows, block)
    return (summed * used.astype(F32))[None]


def solution(mesh):
    placed = (
        P("sector", "pair", None),
        P("pair", "sector", None, None),
        P("pair", "sector", None, None),
        P("pair", "sector"),
        P(),
        P("pair"),
        P(),
    )
    return jax.shard_map(
        body, mesh=mesh, in_specs=placed, out_specs=P("sector", "pair", None), check_vma=False
    )
```

time: 304 us -> 120 us (0.39)
  waiting for transfers between devices: 238 us -> 0 us
  Pallas kernels: 0 us -> 111 us
  local copies, waits for them, and re-layouts: 26.4 us -> 3 us
  between operations: 15.9 us -> 0.04 us
  matrix products: 9.33 us -> 0 us
  other arithmetic: 14 us -> 6.17 us
    reduce_scatter x1 -> x0, waiting for transfers between devices: 193 us -> none  [body(): lax.psum_scatter(arranged, ('pair', 'sector'), scatter_dimension=0, tiled...]
    pallas_call x0 -> x1, Pallas kernels: none -> 111 us  [body(): pl.pallas_call(functools.partial(kernel_entry, cfg), out_shape=jax.ShapeD...]
    all_gather x1 -> x0, waiting for transfers between devices: 44.7 us -> none  [body(): gathered = lax.all_gather(masked, 'pair', axis=0, tiled=True)]
    transpose x1, local copies, waits for them, and re-layouts: 11.8 us -> 1.24 us  [body(): summed = parts.transpose(2, 0, 1, 3).reshape(rows, block)]
    dot_general x1 -> x0, matrix products: 9.33 us -> none  [present_term(): lax.dot_general(left, right_mat, (((1,), (1,)), ((), ())), preferred_elem...]
    dynamic_update_slice x1 -> x0, other arithmetic: 6.77 us -> none  [body(): lax.dynamic_update_index_in_dim(totals, current + addition, place, 0)]
    unnamed x4 -> x0, local copies, waits for them, and re-layouts: 5.77 us -> none
  transfers between devices with their start and end apart: 2 -> 0, of which waited for: 2 -> 0; matrix products, arithmetic and copies ran while one was open for 1% -> 0% of each run, Pallas kernels for 0% -> 0%
where the time goes in v1:
time: 120 us
  Pallas kernels  111 us (92%)
  other arithmetic  6.17 us (5%)
  local copies, waits for them, and re-layouts  3 us (2%)
    pallas_call x1, Pallas kernels, body(): pl.pallas_call(functools.partial(kernel_entry, cfg), out_shape=jax.ShapeD...  111 us

profile of v1, /device:TPU:1, one launch (start us, length us, event | category | flops | bytes accessed | tf_op | source)
XLA Modules:
  0.0 119.7 jit_solution(14219652528688081987)
XLA Ops:
  0.0 1.3 %fusion.1 = s32[]{:T(128)} fusion(s32[4]{0:T(128)} %param.11, s32[]{:T(128)S(6)} %axis_index.25), kind=kLoop, calls=%fused_computation.7 | loop fusion | flops 11 | bytes 24 | tf_op jit(solution)/shard_map/reduce_sum | solution.py:409
  1.3 0.7 add_compare_fusion
  1.9 0.7 iota_compare_fusion
  2.6 0.9 fusion
  3.5 0.7 compare_select_fusion.1
  4.2 0.1 select_n.22
  4.3 0.7 broadcast_in_dim.46.refs_1_
  5.0 1.8 %and_select_fusion.refs_0_ = bf16[128,1024]{1,0:T(8,128)(2,1)} fusion(bf16[1,128,1024]{2,1,0:T(8,128)(2,1)} %param.7, pred[1024]{0:T(1024)(128)(4,1)S(1)} %iota_compare_fusion, pred[128]{0:T(512)(128)(4,1)S(1)} %add_compare_fusion), kind=kLoop, calls=%fused_computation | loop fusion | flops 262144 | bytes 525440 | tf_op jit(solution)/shard_map/mul | solution.py:413
  6.8 110.5 %sigma_step.1 = f32[2,4,128,128]{3,2,1,0:T(8,128)} custom-call(bf16[128,1024]{1,0:T(8,128)(2,1)} %and_select_fusion.refs_0_, f32[8,8,128]{2,1,0:T(8,128)} %broadcast_in_dim.46.refs_1_, bf16[2,1024,1024]{2,1,0:T(8,128)(2,1)} %bitcast.7, bf16[2,1024,1024]{2,1,0:T(8,128)(2,1)} %bitcast.8), custom_call_target="tpu_custom_call" | custom-call | tf_op jit(solution)/shard_map/sigma_step/pallas_call | solution.py:440
  117.3 1.2 %copy.10 = f32[128,2,4,128]{0,3,2,1:T(8,128)S(1)} copy(f32[128,2,4,128]{3,0,2,1:T(8,128)} %bitcast.9) | data formatting | bytes 1048576 | tf_op jit(solution)/shard_map/transpose | solution.py:466
  118.5 0.2 and_select_fusion.1
  118.7 1.0 copy.11

commit v2 on v1

v2 whole, which is shorter than its diff:
```python
import functools

import jax
import jax.numpy as jnp
from jax import lax
from jax.experimental import pallas as pl
from jax.experimental.pallas import tpu as pltpu
from jax.sharding import PartitionSpec as P

MESH = pl.DeviceIdType.MESH
F32 = jnp.float32
LANES = 128
PLANE_DEPTH = 128
ROW_TILE = 256
PIECES = 2


def step_kernel(
    cfg, wave_ref, targets_ref, sizes_ref, ids_ref, coefs_ref, left_hbm, right_hbm, out_ref,
    wbuf, lbuf, rbuf, acc, left, own, psend, precv, weight_ref, wother,
    xs, xr, ys, yr, zs, zr, fsend, frecv, load_sem, sems_s, sems_r, line_s, line_r, gat_s, gat_r,
):
    Z, X, T, K, rows, block, groups, orders = cfg
    half = block // 2
    pair, sector = lax.axis_index("pair"), lax.axis_index("sector")
    z, x = pair // X, lax.rem(pair, X)
    y, c = sector // 2, lax.rem(sector, 2)

    def dev(zz=None, xx=None, yy=None, cc=None):
        zz, xx = z if zz is None else zz, x if xx is None else xx
        yy, cc = y if yy is None else yy, c if cc is None else cc
        return (zz * X + xx, yy * 2 + cc)

    x_dev, y_dev, c_dev = dev(xx=1 - x), dev(yy=1 - y), dev(cc=1 - c)
    up_dev, dn_dev = dev(zz=z + 1), dev(zz=z - 1)

    def loop(count, f):
        def one(i, carry):
            f(i)
            return carry

        lax.fori_loop(0, count, one, 0)

    has_up, has_dn = z + 1 < Z, z >= 1

    loads = []
    for k in range(K):
        loads.append(pltpu.make_async_copy(left_hbm.at[k], lbuf.at[k], load_sem.at[k]))
        loads.append(pltpu.make_async_copy(right_hbm.at[k], rbuf.at[k], load_sem.at[K + k]))
    for k in range(K):
        loads[2 * k].start()

    barrier = pltpu.get_barrier_semaphore()
    for other in (x_dev, y_dev, c_dev):
        pl.semaphore_signal(barrier, inc=1, device_id=other, device_id_type=MESH)

    def greet(zz):
        @pl.when(zz != z)
        def _():
            pl.semaphore_signal(barrier, inc=1, device_id=dev(zz=zz), device_id_type=MESH)

    loop(Z, greet)
    size = sizes_ref[sector]
    row_ids = pair * rows + lax.broadcasted_iota(jnp.int32, (rows, LANES), 0)
    lane_ids = lax.broadcasted_iota(jnp.int32, (rows, LANES), 1)

    def used(column):
        return ((row_ids < size) & (lane_ids + column < size)).astype(F32)

    for at in range(0, block, LANES):
        value = wave_ref[:, at : at + LANES].astype(F32) * used(at)
        wbuf[z, x, :, at : at + LANES] = value.astype(jnp.bfloat16)
    for k in range(K):
        factor = coefs_ref[ids_ref[k]]
        for t in range(T):
            chosen = jnp.where(targets_ref[k, 0] == t, factor, 0.0)
            weight_ref[k * T + t] = jnp.full((8, LANES), chosen, F32)
    for g in range(groups):
        for tc in range(2):
            zr[g][tc, z] = jnp.zeros((rows, LANES), jnp.bfloat16)
    pl.semaphore_wait(barrier, 3 + Z - 1)

    def remote(src, dst, ss, rs, device):
        return pltpu.make_async_remote_copy(
            src_ref=src, dst_ref=dst, send_sem=ss, recv_sem=rs, device_id=device, device_id_type=MESH
        )

    piece = rows // PIECES if rows % (16 * PIECES) == 0 else rows
    pieces = rows // piece

    def block_at(q, xx, p):
        return wbuf.at[q, xx, pl.ds(p * piece, piece)]

    def hop(q, way, p):
        device = (up_dev, dn_dev, x_dev)[way]
        return remote(block_at(q, x, p), block_at(q, x, p), gat_s.at[way, q, p], gat_r.at[q, x, p], device)

    def arrival(q, xx, p):
        return remote(block_at(q, xx, p), block_at(q, xx, p), gat_s.at[2, q, p], gat_r.at[q, xx, p], x_dev)

    def pass_on(q, ways, p):
        if 0 in ways:
            @pl.when(has_up)
            def _():
                hop(q, 0, p).start()

        if 1 in ways:
            @pl.when(has_dn)
            def _():
                hop(q, 1, p).start()

        hop(q, 2, p).start()

    for p in range(pieces):
        pass_on(z, (0, 1), p)
    weights_copy = remote(weight_ref, wother, sems_s.at[0], sems_r.at[0], c_dev)
    weights_copy.start()
    for k in range(K):
        loads[2 * k + 1].start()

    depth = X * rows
    planewise = depth % PLANE_DEPTH == 0
    tile = min(ROW_TILE, block)
    tiles = block // tile

    def multiply(q, first):
        plane = wbuf.at[q]

        def one(i, carry):
            k, at = i // tiles, pl.multiple_of(lax.rem(i, tiles) * tile, tile)
            cols = pl.ds(pl.multiple_of(q * depth, depth), depth)
            product = jnp.dot(
                lbuf[k, pl.ds(at, tile), cols], plane[...].reshape(depth, block), preferred_element_type=F32
            )
            if first:
                acc[k, pl.ds(at, tile), :] = product
            else:
                acc[k, pl.ds(at, tile), :] += product
            return carry

        lax.fori_loop(0, K * tiles, one, 0)

    def take_plane(q, first=False):
        for p in range(pieces):
            arrival(q, 1 - x, p).wait_recv()
        if planewise:
            multiply(q, first)

    for k in range(K):
        loads[2 * k].wait()

    def forward(d, carry):
        lo, hi = z - d, z + d
        for p in range(pieces):
            @pl.when(lo >= 0)
            def _():
                arrival(lo, x, p).wait_recv()
                pass_on(lo, (0,), p)

            @pl.when(hi < Z)
            def _():
                arrival(hi, x, p).wait_recv()
                pass_on(hi, (1,), p)

        @pl.when(d == 1)
        def _():
            take_plane(z, True)

        return carry

    lax.fori_loop(1, Z, forward, 0)

    def take_planes(d, carry):
        @pl.when(z - d >= 0)
        def _():
            take_plane(z - d)

        @pl.when(z + d < Z)
        def _():
            take_plane(z + d)

        return carry

    lax.fori_loop(1, Z, take_planes, 0)

    def finish_left(i, carry):
        k, at = i // tiles, pl.multiple_of(lax.rem(i, tiles) * tile, tile)
        if planewise:
            value = acc[k, pl.ds(at, tile), :]
        else:
            value = jnp.dot(
                lbuf[k, pl.ds(at, tile), :], wbuf[...].reshape(block, block), preferred_element_type=F32
            )
        left[k, pl.ds(at, tile), :] = value.astype(jnp.bfloat16)
        return carry

    lax.fori_loop(0, K * tiles, finish_left, 0)
    for k in range(K):
        loads[2 * k + 1].wait()

    width = 2 * LANES

    def second(part, side, dest):
        def one(i, carry):
            k, at = i // tiles, pl.multiple_of(lax.rem(i, tiles) * tile, tile)
            right_at = pl.multiple_of(side * half + part * width, width)
            term = lax.dot_general(
                left[k, pl.ds(at, tile), :], rbuf[k, pl.ds(right_at, width), :],
                (((1,), (1,)), ((), ())), preferred_element_type=F32,
            )
            for j in range(2):
                dest[2 * part + j, k, pl.ds(at, tile), :] = term[:, j * LANES : (j + 1) * LANES].astype(dest.dtype)
            return carry

        lax.fori_loop(0, K * tiles, one, 0)

    def part_copy(part):
        span = pl.ds(2 * part, 2)
        return remote(psend.at[span], precv.at[span], sems_s.at[1 + part], sems_r.at[1 + part], c_dev)

    base = 1 + groups // 2

    def step_copy(g, number, tc):
        letter = orders[g][number]
        s, r = ((xs, xr), (ys, yr))["xy".index(letter)]
        at = base + 4 * g + 2 * number + tc
        return remote(s[g].at[tc], r[g].at[tc], sems_s.at[at], sems_r.at[at], x_dev if letter == "x" else y_dev)

    def chip_sum(g, ty, tc, zz, xx):
        at = pl.ds(pl.multiple_of((zz * X + xx) * rows, rows), rows)
        t = ty * 2 + tc
        total = None
        for k in range(K):
            mine = own[g, k, at, :] * weight_ref[k * T + t, 0:1, :]
            theirs = precv[g, k, at, :].astype(F32) * wother[k * T + t, 0:1, :]
            total = mine + theirs if total is None else total + mine + theirs
        return total

    def x_first(g, tc):
        def one(zz):
            for ty in range(2):
                xs[g][tc, ty, zz] = chip_sum(g, ty, tc, zz, 1 - x).astype(jnp.bfloat16)

        loop(Z, one)
        step_copy(g, 0, tc).start()

    def y_first(g, tc):
        def one(zz):
            for xx in range(2):
                ys[g][tc, zz, xx] = chip_sum(g, 1 - y, tc, zz, xx).astype(jnp.bfloat16)

        loop(Z, one)
        step_copy(g, 0, tc).start()

    def y_second(g, tc):
        step_copy(g, 0, tc).wait_recv()

        def one(zz):
            value = chip_sum(g, 1 - y, tc, zz, x) + xr[g][tc, 1 - y, zz].astype(F32)
            ys[g][tc, zz] = value.astype(jnp.bfloat16)

        loop(Z, one)
        step_copy(g, 1, tc).start()

    def x_second(g, tc):
        step_copy(g, 0, tc).wait_recv()

        def one(zz):
            value = chip_sum(g, y, tc, zz, 1 - x) + yr[g][tc, zz, 1 - x].astype(F32)
            xs[g][tc, zz] = value.astype(jnp.bfloat16)

        loop(Z, one)
        step_copy(g, 1, tc).start()

    def plane_sum(g, tc, zz):
        value = chip_sum(g, y, tc, zz, x)
        if orders[g][0] == "x":
            return value + xr[g][tc, y, zz].astype(F32) + yr[g][tc, zz].astype(F32)
        return value + yr[g][tc, zz, x].astype(F32) + xr[g][tc, zz].astype(F32)

    def line_copy(g, tc, zz):
        return remote(
            zs[g].at[tc, zz], zr[g].at[tc, z], line_s.at[g, tc, zz], line_r.at[g, tc, z], dev(zz=zz)
        )

    def line_arrival(g, tc, zz):
        return remote(
            zs[g].at[tc, zz], zr[g].at[tc, zz], line_s.at[g, tc, zz], line_r.at[g, tc, zz], dev(zz=zz)
        )

    def line(g, tc):
        step_copy(g, 1, tc).wait_recv()

        def one(j):
            zz = lax.rem(z + 1 + j, Z)
            zs[g][tc, zz] = plane_sum(g, tc, zz).astype(jnp.bfloat16)
            line_copy(g, tc, zz).start()

        loop(Z - 1, one)

    def total(g, tc):
        value = plane_sum(g, tc, z)
        if Z <= 8:
            for zz in range(Z):
                value = value + zr[g][tc, zz].astype(F32)
            return value
        return lax.fori_loop(0, Z, lambda zz, v: v + zr[g][tc, zz].astype(F32), value)

    def final_copy(g):
        at = base + 4 * groups + g
        return remote(fsend.at[g], frecv.at[g], sems_s.at[at], sems_r.at[at], c_dev)

    def finish(g):
        def wait(j):
            for tc in range(2):
                line_arrival(g, tc, lax.rem(z + 1 + j, Z)).wait_recv()

        loop(Z - 1, wait)
        fsend[g] = total(g, 1 - c)
        final_copy(g).start()
        at = pl.multiple_of(c * half + g * LANES, LANES)
        out_ref[:, pl.ds(at, LANES)] = total(g, c) * used(at)

    def first(i):
        x_first(2 * (i // 2), i % 2)
        y_first(2 * (i // 2) + 1, i % 2)

    def next_step(i):
        y_second(2 * (i // 2), i % 2)
        x_second(2 * (i // 2) + 1, i % 2)

    def lines(i):
        line(2 * (i // 2), i % 2)
        line(2 * (i // 2) + 1, i % 2)

    parts = groups // 2
    rounds = groups
    second(0, 1 - c, psend)
    part_copy(0).start()
    second(0, c, own)
    weights_copy.wait_recv()
    for i in range(rounds):
        part = i // 2
        if i % 2 == 0:
            if part + 1 < parts:
                second(part + 1, 1 - c, psend)
                part_copy(part + 1).start()
            part_copy(part).wait_recv()
        first(i)
        if i % 2 == 1 and part + 1 < parts:
            second(part + 1, c, own)
        if i >= 1:
            next_step(i - 1)
        if i >= 2:
            lines(i - 2)
    next_step(rounds - 1)
    lines(rounds - 2)
    for g in range(groups - 2):
        finish(g)
    lines(rounds - 1)
    for g in range(groups - 2, groups):
        finish(g)
    for g in range(groups):
        final_copy(g).wait_recv()
        at = pl.multiple_of((1 - c) * half + g * LANES, LANES)
        out_ref[:, pl.ds(at, LANES)] = frecv[g] * used(at)

    def drain(q):
        for p in range(pieces):
            @pl.when(jnp.logical_and(has_up, q <= z))
            def _():
                hop(q, 0, p).wait_send()

            @pl.when(jnp.logical_and(has_dn, q >= z))
            def _():
                hop(q, 1, p).wait_send()

            hop(q, 2, p).wait_send()

    loop(Z, drain)
    weights_copy.wait_send()
    for part in range(parts):
        part_copy(part).wait_send()
    for g in range(groups):
        final_copy(g).wait_send()
        for tc in range(2):
            step_copy(g, 0, tc).wait_send()
            step_copy(g, 1, tc).wait_send()

            def drain_line(j, g=g, tc=tc):
                line_copy(g, tc, lax.rem(z + 1 + j, Z)).wait_send()

            loop(Z - 1, drain_line)


def kernel_entry(cfg, *refs):
    groups = cfg[6]
    ins, scratch = refs[:8], list(refs[8:])
    plain = scratch[:10]
    per_group = [scratch[10 + n * groups : 10 + (n + 1) * groups] for n in range(6)]
    step_kernel(cfg, *ins, *plain, *per_group, *scratch[10 + 6 * groups :])


def body(wave, left_ops, right_ops, targets, sector_sizes, pair_ids, pair_coefficients):
    block = wave.shape[2]
    rows = wave.shape[1]
    K = left_ops.shape[0]
    T = sector_sizes.shape[0]
    pairs = lax.axis_size("pair")
    X = 2
    Z = pairs // X
    half = block // 2
    groups = half // LANES
    orders = tuple(("xyz", "yxz")[g % 2] for g in range(groups))
    bf = jnp.bfloat16
    xs, xr, ys, yr, zs, zr = [], [], [], [], [], []
    for order in orders:
        tail = (rows, LANES)
        x_shape, y_shape = {"x": ((2, 2, Z), (2, Z)), "y": ((2, Z), (2, Z, X))}[order[0]]
        for where, shape in ((xs, x_shape), (xr, x_shape), (ys, y_shape), (yr, y_shape), (zs, (2, Z)), (zr, (2, Z))):
            where.append(pltpu.VMEM(shape + tail, bf))
    count = 1 + groups // 2 + 5 * groups
    dma = pltpu.SemaphoreType.DMA
    cfg = (Z, X, T, K, rows, block, groups, orders)
    planewise = (X * rows) % PLANE_DEPTH == 0
    vmem, anywhere = pl.BlockSpec(memory_space=pltpu.VMEM), pl.BlockSpec(memory_space=pl.ANY)
    smem = pl.BlockSpec(memory_space=pltpu.SMEM)
    out = pl.pallas_call(
        functools.partial(kernel_entry, cfg),
        out_shape=jax.ShapeDtypeStruct((rows, block), F32),
        in_specs=[vmem, smem, smem, smem, smem, anywhere, anywhere],
        out_specs=vmem,
        scratch_shapes=[
            pltpu.VMEM((Z, X, rows, block), bf),
            pltpu.VMEM((K, block, block), bf),
            pltpu.VMEM((K, block, block), bf),
            pltpu.VMEM((K, block, block) if planewise else (8, LANES), F32),
            pltpu.VMEM((K, block, block), bf),
            pltpu.VMEM((groups, K, block, LANES), F32),
            pltpu.VMEM((groups, K, block, LANES), F32),
            pltpu.VMEM((groups, K, block, LANES), F32),
            pltpu.VMEM((K * T, 8, LANES), F32),
            pltpu.VMEM((K * T, 8, LANES), F32),
            *xs, *xr, *ys, *yr, *zs, *zr,
            pltpu.VMEM((groups, rows, LANES), F32),
            pltpu.VMEM((groups, rows, LANES), F32),
            dma((2 * K,)), dma((count,)), dma((count,)),
            dma((groups, 2, Z)), dma((groups, 2, Z)), dma((3, Z, PIECES)), dma((Z, X, PIECES)),
        ],
        compiler_params=pltpu.CompilerParams(
            collective_id=0, has_side_effects=True, vmem_limit_bytes=60 * 1024 * 1024
        ),
        name="sigma_step",
    )(wave[0], targets, sector_sizes, pair_ids, pair_coefficients, left_ops[:, 0], right_ops[:, 0])
    return out[None]


def solution(mesh):
    placed = (
        P("sector", "pair", None),
        P("pair", "sector", None, None),
        P("pair", "sector", None, None),
        P("pair", "sector"),
        P(),
        P("pair"),
        P(),
    )
    return jax.shard_map(
        body, mesh=mesh, in_specs=placed, out_specs=P("sector", "pair", None), check_vma=False
    )
```

time: 120 us -> 91.4 us (0.76)
  Pallas kernels: 111 us -> 88.1 us
  other arithmetic: 6.17 us -> 0 us
    pallas_call x1, Pallas kernels: 111 us -> 88.1 us  [body(): pl.pallas_call(functools.partial(kernel_entry, cfg), out_shape=jax.ShapeD...]
    unnamed x0 -> x2, local copies, waits for them, and re-layouts: none -> 3.18 us
    reduce_sum x2 -> x0, other arithmetic: 2.15 us -> none  [the longest x1 1.29 us: body(): own_size = jnp.sum(jnp.where(sector_ids == own_sector, sector_sizes, 0))]
    mul x2 -> x0, other arithmetic: 2 us -> none  [the longest x1 1.8 us: body(): masked = wave[0] * used.astype(wave.dtype)]
    lt x2 -> x0, other arithmetic: 1.3 us -> none  [body(): used = (row_ids < own_size)[:, None] & (col_ids < own_size)[None, :]]
    transpose x1 -> x0, local copies, waits for them, and re-layouts: 1.24 us -> none  [body(): summed = parts.transpose(2, 0, 1, 3).reshape(rows, block)]
where the time goes in v2:
time: 91.4 us; the launch traced here: 91.3 us
  Pallas kernels  88.1 us (96%)
  local copies, waits for them, and re-layouts  3.18 us (3%)
    pallas_call x1, Pallas kernels, body(): pl.pallas_call(functools.partial(kernel_entry, cfg), out_shape=jax.ShapeD...  88.1 us
    unnamed x2, local copies, waits for them, and re-layouts  3.18 us

profile of v2, /device:TPU:1, one launch (start us, length us, event | category | flops | bytes accessed | tf_op | source)
XLA Modules:
  0.0 91.3 jit_solution(16261794074096807333)
XLA Ops:
  0.0 1.3 %copy.8.refs_1_ = s32[2,1]{1,0:T(2,128)} copy(s32[2,1]{0,1:T(1,128)} %param.10) | data formatting | bytes 16 | tf_op args[3]
  1.3 88.1 %sigma_step.1 = f32[128,1024]{1,0:T(8,128)} custom-call(bf16[128,1024]{1,0:T(8,128)(2,1)} %bitcast.7, s32[2,1]{1,0:T(2,128)} %copy.8.refs_1_, s32[4]{0:T(128)} %refs_2_.1, s32[2]{0:T(128)} %refs_3_.1, f32[16]{0:T(128)} %refs_4_.1, bf16[2,1024,1024]{2,1,0:T(8,128)(2,1)} %bitcast.4, bf16[2,1024,1024]{2,1,0:T(8,128)(2,1)} %bitcast.5), custom_call_target="tpu_custom_call" | custom-call | tf_op jit(solution)/shard_map/sigma_step/pallas_call | solution.py:428
  89.4 1.9 %copy.10 = f32[1,128,1024]{2,1,0:T(8,128)} copy(f32[1,128,1024]{2,1,0:T(8,128)} %bitcast.6) | data formatting | bytes 1048576

commit v3 on v2

--- a/solution.py
+++ b/solution.py
@@ -11,7 +11,7 @@
 F32 = jnp.float32
 LANES = 128
 PLANE_DEPTH = 128
-ROW_TILE = 256
+ROW_TILE = 512
 PIECES = 2
 
 

time: 91.4 us -> 91.2 us (level)
  no operation moved by 1% of the time
where the time goes in v3:
time: 91.2 us; the launch traced here: 91 us
  Pallas kernels  87.9 us (96%)
  local copies, waits for them, and re-layouts  3.18 us (3%)
    pallas_call x1, Pallas kernels, body(): pl.pallas_call(functools.partial(kernel_entry, cfg), out_shape=jax.ShapeD...  87.9 us
    unnamed x2, local copies, waits for them, and re-layouts  3.18 us

profile of v3, /device:TPU:1, one launch (start us, length us, event | category | flops | bytes accessed | tf_op | source)
XLA Modules:
  0.0 91.0 jit_solution(9135167624313654304)
XLA Ops:
  0.0 1.3 %copy.8.refs_1_ = s32[2,1]{1,0:T(2,128)} copy(s32[2,1]{0,1:T(1,128)} %param.10) | data formatting | bytes 16 | tf_op args[3]
  1.3 87.9 %sigma_step.1 = f32[128,1024]{1,0:T(8,128)} custom-call(bf16[128,1024]{1,0:T(8,128)(2,1)} %bitcast.7, s32[2,1]{1,0:T(2,128)} %copy.8.refs_1_, s32[4]{0:T(128)} %refs_2_.1, s32[2]{0:T(128)} %refs_3_.1, f32[16]{0:T(128)} %refs_4_.1, bf16[2,1024,1024]{2,1,0:T(8,128)(2,1)} %bitcast.4, bf16[2,1024,1024]{2,1,0:T(8,128)(2,1)} %bitcast.5), custom_call_target="tpu_custom_call" | custom-call | tf_op jit(solution)/shard_map/sigma_step/pallas_call | solution.py:428
  89.2 1.9 %copy.10 = f32[1,128,1024]{2,1,0:T(8,128)} copy(f32[1,128,1024]{2,1,0:T(8,128)} %bitcast.6) | data formatting | bytes 1048576
